TPU v7x, 32 devices: a whole 2x2x4 slice. The times are simulated.
32 devices in a mesh: wide: 8 (over y, x, core), narrow: 4 (over z).
Axes of the slice: x: 2, y: 2, z: 4, core: 2. Of those that a mesh axis runs over, the one named last changes fastest.
Arguments:
- panels: float32 [64, 512, 512], P('wide', 'narrow'), may hold values from -0.6 to 0.6
- factors: float32 [16, 512, 512], P('wide', 'narrow'), may hold values from -2 to 2
- member: int32 [16, 4], replicated, may hold values from 0 to 63, as said below
- target: int32 [16, 10], replicated, may hold values from 0 to 7
- ancestors: float32 [8, 512, 512], P('wide', 'narrow'), may hold values from -6 to 6
Outputs:
- updated: float32 [8, 512, 512], P('wide', 'narrow')
Inputs may be any that keep to these rules, and one draw needn't show every extreme that they name: `member`: the blocks of supernode s are 4 distinct indices in [(s // 2) * 8, (s // 2 + 1) * 8); every block belongs to exactly one supernode.
All inputs are finite; a program needn't handle non-finite values.
Results may differ from a plain program's by a relative error of at most 0.0003.
Values sent between devices are 32-bit elements; how exact they have to be, the bound alone decides.
A program may use at most 128 MiB of HBM per device.

v0:
```python
import jax
import jax.numpy as jnp
import numpy as np
from jax import lax
from jax.sharding import PartitionSpec as P


def pair_lists(count):
    left_pick = []
    right_pick = []
    for upper in range(count):
        for lower in range(upper + 1):
            left_pick.append(upper)
            right_pick.append(lower)
    return (np.array(left_pick, dtype=np.int32), np.array(right_pick, dtype=np.int32))


def shards(panels, factors, member, target, ancestors):
    highest = lax.Precision.HIGHEST
    sup_count = factors.shape[0]
    blk_count = panels.shape[0]
    tile_count = ancestors.shape[0] * lax.axis_size("wide")
    left_pick, right_pick = pair_lists(member.shape[1])
    owner_index = lax.axis_index("wide")
    own_members = (
        lax.dynamic_slice_in_dim(member, owner_index * sup_count, sup_count, 0)
        - owner_index * blk_count
    )
    own_targets = lax.dynamic_slice_in_dim(target, owner_index * sup_count, sup_count, 0)
    full_factors = lax.all_gather(factors, "narrow", axis=1, tiled=True)
    blocks = panels[own_members]
    scaled = jnp.einsum("skrw,swv->skrv", blocks, full_factors, precision=highest)
    left_rows = scaled[:, left_pick]
    right_rows = lax.all_gather(scaled, "narrow", axis=2, tiled=True)[:, right_pick]
    updates = jnp.einsum("sprv,spmv->sprm", left_rows, right_rows, precision=highest)
    tile_ids = jnp.arange(tile_count, dtype=jnp.int32)
    onehot = (own_targets[:, :, None] == tile_ids[None, None, :]).astype(jnp.float32)
    portion = jnp.einsum("spa,sprw->arw", onehot, updates, precision=highest)
    totals = lax.psum_scatter(portion, "wide", scatter_dimension=0, tiled=True)
    return ancestors - totals


def solution(mesh):
    return jax.shard_map(
        shards,
        mesh=mesh,
        in_specs=(
            P("wide", "narrow", None),
            P("wide", "narrow", None),
            P(),
            P(),
            P("wide", "narrow", None),
        ),
        out_specs=P("wide", "narrow", None),
        check_vma=False,
    )
```

profile of v0, /device:TPU:1, one launch (start us, length us, event | category | flops | bytes accessed | tf_op | source)
XLA Modules:
  0.0 311.7 jit_solution(10909967429762003381)
XLA Ops:
  6.5 0.0 copy-start
  6.5 0.0 all-gather.3.cloned.1.call-start
  6.5 0.7 all-gather.3.cloned.1.call-update
  7.3 0.0 all-gather.5.cloned.1.call-start
  7.3 0.8 compare_select_fusion
  8.1 0.1 copy.13
  8.2 0.1 reshape.3
  8.3 0.0 copy-done
  8.3 2.0 gather_fusion
  10.3 46.2 %all-gather.3.cloned.1.call-done = f32[2,512,512]{2,1,0:T(8,128)} async-done(((f32[2,128,512]{2,1,0:T(8,128)}), f32[2,512,512]{2,1,0:T(8,128)}) %all-gather.3.cloned.1.call-update) | async-done | bytes 2097168 | tf_op jit(solution)/shard_map/all_gather | solution.py:30
  56.5 7.1 %fusion.5 = f32[2,4,128,512]{3,2,1,0:T(8,128)} fusion(f32[2,4,128,512]{3,2,1,0:T(8,128)} %bitcast.21, f32[2,512,512]{2,1,0:T(8,128)} %all-gather.3.cloned.1.call-done), kind=kOutput, calls=%fused_computation.8 | convolution fusion | flops 3221225472 | bytes 6291456 | tf_op jit(solution)/shard_map/skrw,swv->skrv/dot_general | solution.py:32
  63.6 0.0 all-gather.5.cloned.1.call-update
  63.6 0.2 reduce-scatter.2.cloned.1.call-start
  63.8 0.7 constant_dynamic-slice_fusion
  64.5 4.8 %gather_fusion.1 = f32[10,2,128,512]{3,2,1,0:T(8,128)} fusion(f32[2,4,128,512]{3,2,1,0:T(8,128)} %fusion.5, s32[1024]{0:T(1024)S(1)} %pad_clamp_fusion.1), kind=kCustom, calls=%fused_computation.1 | custom fusion | bytes 10485800 | tf_op jit(solution)/shard_map/gather | solution.py:33
  69.3 143.2 %all-gather.5.cloned.1.call-done = f32[2,4,512,512]{3,2,1,0:T(8,128)} async-done(((f32[2,4,128,512]{3,2,1,0:T(8,128)}), f32[2,4,512,512]{3,2,1,0:T(8,128)}) %all-gather.5.cloned.1.call-update) | async-done | bytes 8388624 | tf_op jit(solution)/shard_map/all_gather | solution.py:34
  212.5 12.6 %gather_fusion.2 = f32[10,2,512,512]{3,2,1,0:T(8,128)} fusion(f32[2,4,512,512]{3,2,1,0:T(8,128)} %all-gather.5.cloned.1.call-done, s32[1024]{0:T(1024)S(1)} %pad_clamp_fusion), kind=kCustom, calls=%fused_computation.2 | custom fusion | bytes 41943080 | tf_op jit(solution)/shard_map/gather | solution.py:34
  225.1 28.1 %fusion = f32[2,10,128,512]{3,2,1,0:T(8,128)} fusion(f32[10,2,512,512]{3,2,1,0:T(8,128)} %gather_fusion.2, f32[10,2,128,512]{3,2,1,0:T(8,128)} %gather_fusion.1), kind=kOutput, calls=%fused_computation.3 | convolution fusion | flops 8053063680 | bytes 31457280 | tf_op jit(solution)/shard_map/sprv,spmv->sprm/dot_general | solution.py:35
  253.2 8.6 %fusion.7 = f32[8,128,512]{2,0,1:T(8,128)S(1)} fusion(f32[2,10,128,512]{3,2,1,0:T(8,128)} %fusion, s32[2,10]{1,0:T(2,128)S(1)} %constant_dynamic-slice_fusion), kind=kOutput, calls=%fused_computation.10 | convolution fusion | flops 125829280 | bytes 7340112 | tf_op jit(solution)/shard_map/spa,sprw->arw/dot_general | solution.py:38
  261.8 0.0 copy-start.1
  261.8 2.6 copy.14
  264.4 0.0 reduce-scatter.2.cloned.1.call-update
  264.4 39.1 %reduce-scatter.2.cloned.1.call-done = f32[1,128,512]{2,1,0:T(8,128)} async-done(((f32[8,128,512]{2,1,0:T(8,128)}), f32[1,128,512]{2,1,0:T(8,128)}) %reduce-scatter.2.cloned.1.call-update) | async-done | bytes 262160 | tf_op jit(solution)/shard_map/reduce_scatter | solution.py:39
  303.5 1.7 sub.11
  (8 shorter events, 0.0 us)
Async XLA Ops:
  6.5 1.7 copy-start
  6.5 50.0 %all-gather.3.cloned.1.call-start = ((), (), s32[]{:S(2)}) async-start(), calls=%async_computation.1 | async-start | bytes 2621440 | tf_op jit(solution)/shard_map/all_gather | solution.py:30
  7.3 205.2 %all-gather.5.cloned.1.call-start = ((), (), s32[]{:S(2)}) async-start(), calls=%async_computation.2 | async-start | bytes 10485760 | tf_op jit(solution)/shard_map/all_gather | solution.py:34
  10.3 54.2 %copy-start.3 = (s32[10]{0:T(128)S(1)}, s32[10]{0:T(128)}, u32[]{:S(2)}) copy-start(s32[10]{0:T(128)} %constant.32) | copy-start | bytes 124
  10.3 54.3 %copy-start.2 = (s32[10]{0:T(128)S(1)}, s32[10]{0:T(128)}, u32[]{:S(2)}) copy-start(s32[10]{0:T(128)} %constant.31) | copy-start | bytes 124
  63.6 239.9 %reduce-scatter.2.cloned.1.call-start = ((), (), s32[]{:S(2)}) async-start(), calls=%async_computation.3 | async-start | bytes 2359296 | tf_op jit(solution)/shard_map/reduce_scatter | solution.py:39
  261.8 41.7 %copy-start.1 = (f32[1,128,512]{2,1,0:T(8,128)S(1)}, f32[1,128,512]{2,1,0:T(8,128)}, u32[]{:S(2)}) copy-start(f32[1,128,512]{2,1,0:T(8,128)} %param.13) | copy-start | bytes 786436
Sparse Core Ops, SparseCore 0:
  8.9 47.5 all-gather.2
  63.7 148.7 all-gather.4
  264.5 38.9 reduce-scatter.1
where the time goes:
time: 313 us; the launch traced here: 312 us
  waiting for transfers between devices  229 us (73%)
  matrix products  43.8 us (14%)
  local copies, waits for them, and re-layouts  22.8 us (7%)
  between operations  13.2 us (4%)
    all_gather x1, waiting for transfers between devices, shards(): lax.all_gather(scaled, 'narrow', axis=2, tiled=True)[:, right_pick]  143 us
    all_gather x1, waiting for transfers between devices, shards(): full_factors = lax.all_gather(factors, 'narrow', axis=1, tiled=True)  46.2 us
    reduce_scatter x1, waiting for transfers between devices, shards(): totals = lax.psum_scatter(portion, 'wide', scatter_dimension=0, tiled=True)  39.1 us
    dot_general x1, matrix products, shards(): jnp.einsum('sprv,spmv->sprm', left_rows, right_rows, precision=highest)  28.1 us
    gather x1, local copies, waits for them, and re-layouts, shards(): lax.all_gather(scaled, 'narrow', axis=2, tiled=True)[:, right_pick]  12.6 us
    dot_general x1, matrix products, shards(): portion = jnp.einsum('spa,sprw->arw', onehot, updates, precision=highest)  8.61 us
    dot_general x1, matrix products, shards(): jnp.einsum('skrw,swv->skrv', blocks, full_factors, precision=highest)  7.07 us
  transfers between devices with their start and end apart: 3, of which 3 were waited for; matrix products, arithmetic and copies ran while one was open for 3% of the time, Pallas kernels for 0%

commit v1 on v0

v1 whole, which is shorter than its diff:
```python
import functools

import jax
import jax.numpy as jnp
from jax import lax
from jax.experimental import pallas as pl
from jax.experimental.pallas import tpu as pltpu
from jax.sharding import PartitionSpec as P

MESH = pl.DeviceIdType.MESH
CORES = 2
ROWS_DOT = (((1,), (1,)), ((), ()))
COLS_DOT = (((1,), (0,)), ((), ()))


def halves(x):
    hi = x.astype(jnp.bfloat16)
    return hi, (x - hi.astype(jnp.float32)).astype(jnp.bfloat16)


def dot3(ah, al, bh, bl, dims):
    dot = functools.partial(
        lax.dot_general, dimension_numbers=dims, preferred_element_type=jnp.float32
    )
    return dot(ah, bh) + (dot(ah, bl) + dot(al, bh))


def kernel(cfg, weight, blocks, factors, ancestors, out, p_recv, f_full, fh, fl, s_full, s_hi, s_lo,
           upd, portion, xy_recv, zsum, z_recv, loc_sem, fs_sem, fr_sem, f2s_sem, f2r_sem, ps_sem, pr_sem,
           ss_sem, sr_sem, xs_sem, xr_sem, zs_sem, zr_sem):
    n, q_count, sups, nb, width, part, unit, split = cfg
    wide = lax.axis_index("wide")
    z = lax.axis_index("narrow")
    core = lax.rem(wide, CORES)
    q = lax.div(wide, CORES)
    mine = lax.rem(z, unit) * CORES + core
    my_unit = lax.div(z, unit)
    src_core = lax.div(my_unit, sups)

    def at(q_, core_, z_):
        return {"wide": q_ * CORES + core_, "narrow": z_}

    barrier = pltpu.get_barrier_semaphore()
    for i in range(1, CORES * n):
        other = lax.rem(z * CORES + core + i, CORES * n)
        pl.semaphore_signal(barrier, inc=1, device_id=at(q, lax.rem(other, CORES), lax.div(other, CORES)),
                            device_id_type=MESH)
    for i in range(1, q_count):
        pl.semaphore_signal(barrier, inc=1, device_id=at(lax.rem(q + i, q_count), core, z), device_id_type=MESH)
    pl.semaphore_wait(barrier, CORES * n - 1 + q_count - 1)

    anc_copy = pltpu.make_async_copy(ancestors.at[0], out.at[0], loc_sem)
    anc_copy.start()

    def remote(src, dst, send, recv, dev):
        return pltpu.make_async_remote_copy(src_ref=src, dst_ref=dst, send_sem=send, recv_sem=recv,
                                            device_id=dev, device_id_type=MESH)

    def source_copies(what, i):
        s, e = i // split, i % split
        chip = (core * sups + s) * unit + e // CORES
        to_self = jnp.logical_and(chip == z, core == e % CORES)
        rows = pl.ds(e * part, part)
        if what == "f":
            src, dst, ssem, rsem = factors.at[s, rows], f_full.at[z, e], fs_sem.at[i], fr_sem.at[z]
        else:
            src, dst, ssem, rsem = blocks.at[s, :, rows], p_recv.at[z], ps_sem.at[i], pr_sem.at[z]
        return to_self, pltpu.make_async_copy(src, dst, rsem), remote(src, dst, ssem, rsem, at(q, e % CORES, chip))

    for what in ("f", "p"):
        for i in range(sups * split):
            to_self, local, away = source_copies(what, i)
            pl.when(to_self)(local.start)
            pl.when(jnp.logical_not(to_self))(away.start)

    def arrived(ref, sem):
        pltpu.make_async_copy(ref, ref, sem).wait()

    for i in range(n):
        arrived(f_full.at[i, mine], fr_sem.at[i])

    def peer(i):
        other = lax.rem(mine + i, split)
        return other, at(q, lax.rem(other, CORES), my_unit * unit + lax.div(other, CORES))

    f_copies = []
    for i in range(1, split):
        other, dev = peer(i)
        f_copies.append(remote(f_full.at[:, mine], f_full.at[:, mine], f2s_sem.at[other], f2r_sem.at[mine], dev))
        f_copies[-1].start()
    for i in range(1, split):
        other, dev = peer(i)
        arrived(f_full.at[:, other], f2r_sem.at[other])
    hi, lo = halves(f_full[...].reshape(width, width))
    fh[...] = hi
    fl[...] = lo

    def scale(i, carry):
        zz = lax.rem(z + i, n)
        arrived(p_recv.at[zz], pr_sem.at[zz])
        ph, plo = halves(p_recv[zz].reshape(nb * part, width))
        s = dot3(ph, plo, fh[...], fl[...], COLS_DOT).reshape(nb, part, width)
        s_full[:, zz, mine] = s
        for j in range(1, split):
            other, dev = peer(j)
            remote(s_full.at[:, zz, mine], s_full.at[:, zz, mine], ss_sem.at[zz, other],
                   sr_sem.at[zz, mine], dev).start()
        sh, sl = halves(s)
        s_hi[:, zz, mine] = sh
        s_lo[:, zz, mine] = sl
        return carry

    lax.fori_loop(0, n, scale, 0)

    def take(i, carry):
        zz = lax.rem(z + i, n)
        for j in range(1, split):
            other, dev = peer(j)
            arrived(s_full.at[:, zz, other], sr_sem.at[zz, other])
            sh, sl = halves(s_full[:, zz, other])
            s_hi[:, zz, other] = sh
            s_lo[:, zz, other] = sl
        return carry

    lax.fori_loop(0, n, take, 0)

    for k in range(nb):
        def update(l, carry, k=k):
            u = dot3(s_hi[k, :, mine].reshape(n * part, width), s_lo[k, :, mine].reshape(n * part, width),
                     s_hi[l].reshape(width, width), s_lo[l].reshape(width, width), ROWS_DOT)
            upd[k * (k + 1) // 2 + l] = u.reshape(n, part, width)
            return carry

        lax.fori_loop(0, k + 1, update, 0)

    pairs = nb * (nb + 1) // 2
    step = 8

    def group(i):
        return lax.rem(z + n // 2 + i, n)

    def xy_copy(zz, other):
        pair = pl.ds(other * CORES, CORES)
        return remote(portion.at[pair, zz], xy_recv.at[q, :, zz], xs_sem.at[other, zz], xr_sem.at[q, zz],
                      at(other, core, z))

    def tiles(i, carry):
        zz = group(lax.div(i, q_count))
        other = lax.rem(q + 1 + lax.rem(i, q_count), q_count)

        def rows(r, inner):
            at_rows = pl.ds(pl.multiple_of(r * step, step), step)
            parts = [upd[p, zz, at_rows] for p in range(pairs)]
            for c in range(CORES):
                tile = other * CORES + c
                portion[tile, zz, at_rows] = sum(weight[tile, p] * parts[p] for p in range(pairs))
            return inner

        lax.fori_loop(0, part // step, rows, 0)

        @pl.when(other != q)
        def _():
            xy_copy(zz, other).start()

        return carry

    lax.fori_loop(0, n * q_count, tiles, 0)

    def z_copy(zz, c):
        return remote(zsum.at[zz, c], z_recv.at[z, core], zs_sem.at[zz, c], zr_sem.at[z, core], at(q, c, zz))

    def gather(i, carry):
        zz = group(i)
        for j in range(1, q_count):
            other = lax.rem(q + j, q_count)
            arrived(xy_recv.at[other, :, zz], xr_sem.at[other, zz])
        total = portion[pl.ds(q * CORES, CORES), zz]
        for j in range(1, q_count):
            total = total + xy_recv[lax.rem(q + j, q_count), :, zz]
        zsum[zz] = total
        for c in range(CORES):
            own = jnp.logical_and(zz == z, core == c)

            @pl.when(own)
            def _():
                z_recv[z, core] = total[c]

            @pl.when(jnp.logical_not(own))
            def _():
                z_copy(zz, c).start()

        return carry

    lax.fori_loop(0, n, gather, 0)

    for i in range(1, CORES * n):
        other = lax.rem(z * CORES + core + i, CORES * n)
        oz, oc = lax.div(other, CORES), lax.rem(other, CORES)
        arrived(z_recv.at[oz, oc], zr_sem.at[oz, oc])
    anc_copy.wait()
    for e in range(split):
        rows = pl.ds(e * part, part)
        out[0, rows] = out[0, rows] - sum(z_recv[u * unit + e // CORES, e % CORES] for u in range(n // unit))

    for what in ("f", "p"):
        for i in range(sups * split):
            to_self, local, away = source_copies(what, i)
            pl.when(jnp.logical_not(to_self))(away.wait_send)
    for copy in f_copies:
        copy.wait_send()

    def sent(i, carry):
        for j in range(1, split):
            other, dev = peer(j)
            remote(s_full.at[:, i, mine], s_full.at[:, i, mine], ss_sem.at[i, other],
                   sr_sem.at[i, mine], dev).wait_send()
        for j in range(1, q_count):
            xy_copy(i, lax.rem(q + j, q_count)).wait_send()
        for c in range(CORES):
            @pl.when(jnp.logical_not(jnp.logical_and(i == z, core == c)))
            def _():
                z_copy(i, c).wait_send()
        return carry

    lax.fori_loop(0, n, sent, 0)


def shards(panels, factors, member, target, ancestors):
    sups, blk_count, nb = factors.shape[0], panels.shape[0], member.shape[1]
    width = panels.shape[2]
    n, wide_count = lax.axis_size("narrow"), lax.axis_size("wide")
    q_count = wide_count // CORES
    tile_count = ancestors.shape[0] * wide_count
    assert ancestors.shape[0] == 1 and n % (CORES * sups) == 0
    unit = n // (CORES * sups)
    split = unit * CORES
    part = panels.shape[1] // split
    wide, z = lax.axis_index("wide"), lax.axis_index("narrow")
    own_members = lax.dynamic_slice_in_dim(member, wide * sups, sups, 0) - wide * blk_count
    blocks = panels[own_members]
    supernode = (wide // CORES) * (CORES * sups) + z // unit
    own_targets = lax.dynamic_slice_in_dim(target, supernode, 1, 0)
    weight = (own_targets == jnp.arange(tile_count, dtype=jnp.int32)[:, None]).astype(jnp.float32)
    pairs = target.shape[1]
    f32, bf16 = jnp.float32, jnp.bfloat16
    dma = pltpu.SemaphoreType.DMA
    cfg = (n, q_count, sups, nb, width, part, unit, split)
    any_space = pl.BlockSpec(memory_space=pl.ANY)
    return pl.pallas_call(
        functools.partial(kernel, cfg),
        out_shape=jax.ShapeDtypeStruct(ancestors.shape, f32),
        in_specs=[pl.BlockSpec(memory_space=pltpu.SMEM), any_space, any_space, any_space],
        out_specs=pl.BlockSpec(memory_space=pltpu.VMEM),
        scratch_shapes=[
            pltpu.VMEM((n, nb, part, width), f32),
            pltpu.VMEM((n, split, part, width), f32),
            pltpu.VMEM((width, width), bf16),
            pltpu.VMEM((width, width), bf16),
            pltpu.VMEM((nb, n, split, part, width), f32),
            pltpu.VMEM((nb, n, split, part, width), bf16),
            pltpu.VMEM((nb, n, split, part, width), bf16),
            pltpu.VMEM((pairs, n, part, width), f32),
            pltpu.VMEM((tile_count, n, part, width), f32),
            pltpu.VMEM((q_count, CORES, n, part, width), f32),
            pltpu.VMEM((n, CORES, part, width), f32),
            pltpu.VMEM((n, CORES, part, width), f32),
            dma,
            dma((sups * split,)), dma((n,)),
            dma((split,)), dma((split,)),
            dma((sups * split,)), dma((n,)),
            dma((n, split)), dma((n, split)),
            dma((q_count, n)), dma((q_count, n)),
            dma((n, CORES)), dma((n, CORES)),
        ],
        compiler_params=pltpu.CompilerParams(
            collective_id=0, has_side_effects=True, vmem_limit_bytes=58 * 2**20
        ),
        name="level",
    )(weight, blocks, factors, ancestors)


def solution(mesh):
    return jax.shard_map(
        shards,
        mesh=mesh,
        in_specs=(
            P("wide", "narrow", None),
            P("wide", "narrow", None),
            P(),
            P(),
            P("wide", "narrow", None),
        ),
        out_specs=P("wide", "narrow", None),
        check_vma=False,
    )
```

time: 313 us -> 135 us (0.43)
  waiting for transfers between devices: 229 us -> 0 us
  Pallas kernels: 0 us -> 129 us
  matrix products: 43.8 us -> 0 us
  local copies, waits for them, and re-layouts: 22.8 us -> 4.72 us
  between operations: 13.2 us -> 0.01 us
    all_gather x2 -> x0, waiting for transfers between devices: 189 us -> none  [the longest x1 143 us: shards(): lax.all_gather(scaled, 'narrow', axis=2, tiled=True)[:, right_pick]]
    pallas_call x0 -> x1, Pallas kernels: none -> 129 us  [shards(): pl.pallas_call(functools.partial(kernel, cfg), out_shape=jax.ShapeDtypeSt...]
    dot_general x3 -> x0, matrix products: 43.8 us -> none  [the longest x1 28.1 us: shards(): jnp.einsum('sprv,spmv->sprm', left_rows, right_rows, precision=highest)]
    reduce_scatter x1 -> x0, waiting for transfers between devices: 39.1 us -> none  [shards(): totals = lax.psum_scatter(portion, 'wide', scatter_dimension=0, tiled=True)]
    gather x2 -> x0, local copies, waits for them, and re-layouts: 17.4 us -> none  [the longest x1 12.6 us: shards(): lax.all_gather(scaled, 'narrow', axis=2, tiled=True)[:, right_pick]]
  transfers between devices with their start and end apart: 3 -> 0, of which waited for: 3 -> 0; matrix products, arithmetic and copies ran while one was open for 3% -> 0% of each run, Pallas kernels for 0% -> 0%
where the time goes in v1:
time: 135 us
  Pallas kernels  129 us (96%)
  local copies, waits for them, and re-layouts  4.72 us (3%)
  other arithmetic  1.36 us (1%)
    pallas_call x1, Pallas kernels, shards(): pl.pallas_call(functools.partial(kernel, cfg), out_shape=jax.ShapeDtypeSt...  129 us

profile of v1, /device:TPU:1, one launch (start us, length us, event | category | flops | bytes accessed | tf_op | source)
XLA Modules:
  0.0 134.6 jit_solution(10220666901829836059)
XLA Ops:
  0.0 0.0 copy-start
  0.0 0.8 dynamic-slice_bitcast_fusion
  0.8 0.8 compare_select_fusion
  1.6 0.1 copy.6
  1.7 0.1 reshape.2
  1.8 0.6 fusion.weight
  2.4 0.0 copy-done
  2.4 2.0 %gather_fusion = f32[8,128,512]{2,1,0:T(8,128)} fusion(f32[8,128,512]{2,1,0:T(8,128)S(1)} %copy-done, s32[1024]{0:T(1024)S(1)} %pad_clamp_fusion), kind=kCustom, calls=%fused_computation | custom fusion | bytes 4194336 | tf_op jit(solution)/shard_map/gather | solution.py:240
  4.4 128.5 %level.1 = f32[1,128,512]{2,1,0:T(8,128)} custom-call(f32[8,10]{1,0:T(8,128)} %fusion.weight, f32[2,4,128,512]{3,2,1,0:T(8,128)} %bitcast.3, f32[2,128,512]{2,1,0:T(8,128)} %factors.1, f32[1,128,512]{2,1,0:T(8,128)} %ancestors.1), custom_call_target="tpu_custom_call" | custom-call | tf_op jit(solution)/shard_map/level/pallas_call | solution.py:249
  132.9 1.7 %copy.8 = f32[1,128,512]{2,1,0:T(8,128)} copy(f32[1,128,512]{2,1,0:T(8,128)} %level.1) | data formatting | bytes 524288
  (1 shorter events, 0.0 us)
Async XLA Ops:
  0.0 2.4 %copy-start = (f32[8,128,512]{2,1,0:T(8,128)S(1)}, f32[8,128,512]{2,1,0:T(8,128)}, u32[]{:S(2)}) copy-start(f32[8,128,512]{2,1,0:T(8,128)} %param.5) | copy-start | bytes 6291460

commit v2 on v1

v2 whole, which is shorter than its diff:
```python
import functools

import jax
import jax.numpy as jnp
from jax import lax
from jax.experimental import pallas as pl
from jax.experimental.pallas import tpu as pltpu
from jax.sharding import PartitionSpec as P

MESH = pl.DeviceIdType.MESH
CORES = 2
ROWS_DOT = (((1,), (1,)), ((), ()))
COLS_DOT = (((1,), (0,)), ((), ()))


def halves(x):
    hi = x.astype(jnp.bfloat16)
    return hi, (x - hi.astype(jnp.float32)).astype(jnp.bfloat16)


def dot3(ah, al, bh, bl, dims):
    dot = functools.partial(
        lax.dot_general, dimension_numbers=dims, preferred_element_type=jnp.float32
    )
    return dot(ah, bh) + (dot(ah, bl) + dot(al, bh))


def kernel(cfg, weight, blocks, factors, ancestors, out, p_recv, f_full, fh, fl, s_full, s_hi, s_lo,
           upd, portion, xy_recv, zsum, z_recv, loc_sem, fs_sem, fr_sem, f2s_sem, f2r_sem, ps_sem, pr_sem,
           ss_sem, sr_sem, xs_sem, xr_sem, zs_sem, zr_sem, turn_sem):
    n, q_count, sups, nb, width, part, unit, split = cfg
    units = CORES * sups
    mid = units // 2
    rows_own = unit * part
    cols = width // units
    wide = lax.axis_index("wide")
    z = lax.axis_index("narrow")
    core = lax.rem(wide, CORES)
    q = lax.div(wide, CORES)
    mine = lax.rem(z, unit) * CORES + core
    my_unit = lax.div(z, unit)
    half = lax.div(my_unit, mid)
    far_sender = core != half

    def at(q_, core_, z_):
        return {"wide": q_ * CORES + core_, "narrow": z_}

    def order(i):
        h, j = i // mid, i % mid
        near = half * mid + lax.rem(my_unit - half * mid + j, mid)
        far = mid + j - half * (1 + 2 * j)
        return (1 - h) * near + h * far

    barrier = pltpu.get_barrier_semaphore()
    for i in range(1, CORES * n):
        other = lax.rem(z * CORES + core + i, CORES * n)
        pl.semaphore_signal(barrier, inc=1, device_id=at(q, lax.rem(other, CORES), lax.div(other, CORES)),
                            device_id_type=MESH)
    for i in range(1, q_count):
        pl.semaphore_signal(barrier, inc=1, device_id=at(lax.rem(q + i, q_count), core, z), device_id_type=MESH)
    pl.semaphore_wait(barrier, CORES * n - 1 + q_count - 1)

    anc_copy = pltpu.make_async_copy(ancestors.at[0], out.at[0], loc_sem)
    anc_copy.start()

    def remote(src, dst, send, recv, dev):
        return pltpu.make_async_remote_copy(src_ref=src, dst_ref=dst, send_sem=send, recv_sem=recv,
                                            device_id=dev, device_id_type=MESH)

    def source_copy(what, i, local):
        s, e = i // split, i % split
        chip = (core * sups + s) * unit + e // CORES
        rows = pl.ds(e * part, part)
        if what == "f":
            src, dst, ssem, rsem = factors.at[s, rows], f_full.at[z, e], fs_sem.at[i], fr_sem.at[z]
        else:
            src, dst, ssem, rsem = blocks.at[s, :, rows], p_recv.at[z], ps_sem.at[i], pr_sem.at[z]
        if local:
            return pltpu.make_async_copy(src, dst, rsem)
        return remote(src, dst, ssem, rsem, at(q, e % CORES, chip))

    def to_self(i):
        s, e = i // split, i % split
        return jnp.logical_and((core * sups + s) * unit + e // CORES == z, core == e % CORES)

    def send_all(what):
        for i in range(sups * split):
            @pl.when(to_self(i))
            def _():
                source_copy(what, i, True).start()

            @pl.when(jnp.logical_not(to_self(i)))
            def _():
                source_copy(what, i, False).start()

    inner = jnp.logical_or(my_unit == mid - 1, my_unit == mid)
    outer_unit = half * (units - 1)
    outer_far = jnp.logical_and(far_sender, my_unit == outer_unit)
    inner_far = jnp.logical_and(far_sender, inner)
    send_all("f")
    pl.when(jnp.logical_not(outer_far))(lambda: send_all("p"))

    def arrived(ref, sem):
        pltpu.make_async_copy(ref, ref, sem).wait()

    for i in range(n):
        arrived(f_full.at[i, mine], fr_sem.at[i])

    def peer(i):
        other = lax.rem(mine + i, split)
        return other, at(q, lax.rem(other, CORES), my_unit * unit + lax.div(other, CORES))

    f_copies = []
    for i in range(1, split):
        other, dev = peer(i)
        f_copies.append(remote(f_full.at[:, mine], f_full.at[:, mine], f2s_sem.at[other], f2r_sem.at[mine], dev))
        f_copies[-1].start()
    for i in range(1, split):
        other, dev = peer(i)
        arrived(f_full.at[:, other], f2r_sem.at[other])
    hi, lo = halves(f_full[...].reshape(width, width))
    fh[...] = hi
    fl[...] = lo

    def s_copy(zz, j):
        other, dev = peer(j)
        return remote(s_full.at[:, zz, mine], s_full.at[:, zz, mine], ss_sem.at[zz, other],
                      sr_sem.at[zz, mine], dev)

    def scale(a):
        for m in range(unit):
            zz = a * unit + m
            arrived(p_recv.at[zz], pr_sem.at[zz])
            ph, plo = halves(p_recv[zz].reshape(nb * part, width))
            s = dot3(ph, plo, fh[...], fl[...], COLS_DOT).reshape(nb, part, width)
            s_full[:, zz, mine] = s
            for j in range(1, split):
                s_copy(zz, j).start()
            sh, sl = halves(s)
            s_hi[:, zz, mine] = sh
            s_lo[:, zz, mine] = sl
        for m in range(unit):
            zz = a * unit + m
            for j in range(1, split):
                other, dev = peer(j)
                arrived(s_full.at[:, zz, other], sr_sem.at[zz, other])
                sh, sl = halves(s_full[:, zz, other])
                s_hi[:, zz, other] = sh
                s_lo[:, zz, other] = sl

    def xy_copy(a, b, other):
        return remote(portion.at[a, b, pl.ds(other * CORES, CORES)], xy_recv.at[q, a, b],
                      xs_sem.at[other, a, b], xr_sem.at[q, a, b], at(other, core, z))

    lefts = nb // 2

    def block(a, b):
        az, bz = pl.ds(a * unit, unit), pl.ds(b * unit, unit)
        for first in range(0, nb, lefts):
            ks, ls = pl.ds(first, nb - first), pl.ds(first, lefts)
            left = [r[ks, az, mine].reshape((nb - first) * rows_own, width) for r in (s_hi, s_lo)]
            right = [r[ls, bz].reshape(lefts * cols, width) for r in (s_hi, s_lo)]
            upd[first * rows_own:, first * cols:(first + lefts) * cols] = dot3(*left, *right, ROWS_DOT)

        def tiles(i, carry):
            other = lax.rem(q + 1 + i, q_count)
            sums = [None] * CORES
            p = 0
            for k in range(nb):
                for l in range(k + 1):
                    u = upd[k * rows_own:(k + 1) * rows_own, l * cols:(l + 1) * cols]
                    for c in range(CORES):
                        term = weight[other * CORES + c, p] * u
                        sums[c] = term if p == 0 else sums[c] + term
                    p += 1
            for c in range(CORES):
                portion[a, b, other * CORES + c] = sums[c]

            @pl.when(other != q)
            def _():
                xy_copy(a, b, other).start()

            return carry

        lax.fori_loop(0, q_count, tiles, 0)

    for i in range(units):
        if i == mid:
            @pl.when(inner_far)
            def _():
                for j in range(sups * split):
                    source_copy("p", j, False).wait_send()
                pl.semaphore_signal(turn_sem, inc=1, device_id=at(q, core, z - unit + 2 * unit * half),
                                    device_id_type=MESH)

            @pl.when(outer_far)
            def _():
                pl.semaphore_wait(turn_sem, 1)
                send_all("p")

        new = order(i)
        scale(new)

        def blocks_of(j, carry, i=i, new=new):
            old = jnp.minimum(j, i)
            row = order(old)
            block(row, order(jnp.where(j < i, i, j - i)))
            return carry

        lax.fori_loop(0, 2 * i + 1, blocks_of, 0)

    def z_copy(zz, c):
        return remote(zsum.at[zz, c], z_recv.at[z, core], zs_sem.at[zz, c], zr_sem.at[z, core], at(q, c, zz))

    def gather(i, carry):
        a = order(i)
        for b in range(units):
            total = portion[a, b, pl.ds(q * CORES, CORES)]
            for j in range(1, q_count):
                other = lax.rem(q + j, q_count)
                arrived(xy_recv.at[other, a, b], xr_sem.at[other, a, b])
                total = total + xy_recv[other, a, b]
            for m in range(unit):
                zsum[a * unit + m, :, :, b * cols:(b + 1) * cols] = total[:, m * part:(m + 1) * part]
        for m in range(unit):
            zz = a * unit + m
            for c in range(CORES):
                own = jnp.logical_and(zz == z, core == c)

                @pl.when(own)
                def _():
                    z_recv[z, core] = zsum[zz, c]

                @pl.when(jnp.logical_not(own))
                def _():
                    z_copy(zz, c).start()

        return carry

    lax.fori_loop(0, units, gather, 0)

    for i in range(1, CORES * n):
        other = lax.rem(z * CORES + core + i, CORES * n)
        oz, oc = lax.div(other, CORES), lax.rem(other, CORES)
        arrived(z_recv.at[oz, oc], zr_sem.at[oz, oc])
    anc_copy.wait()
    for e in range(split):
        rows = pl.ds(e * part, part)
        out[0, rows] = out[0, rows] - sum(z_recv[u * unit + e // CORES, e % CORES] for u in range(n // unit))

    for i in range(sups * split):
        @pl.when(jnp.logical_not(to_self(i)))
        def _():
            source_copy("f", i, False).wait_send()

        @pl.when(jnp.logical_not(jnp.logical_or(to_self(i), inner_far)))
        def _():
            source_copy("p", i, False).wait_send()
    for copy in f_copies:
        copy.wait_send()

    def sent(i, carry):
        for j in range(1, split):
            s_copy(i, j).wait_send()
        for c in range(CORES):
            @pl.when(jnp.logical_not(jnp.logical_and(i == z, core == c)))
            def _():
                z_copy(i, c).wait_send()
        return carry

    lax.fori_loop(0, n, sent, 0)

    def sent_xy(i, carry):
        for j in range(1, q_count):
            xy_copy(i // units, i % units, lax.rem(q + j, q_count)).wait_send()
        return carry

    lax.fori_loop(0, units * units, sent_xy, 0)


def shards(panels, factors, member, target, ancestors):
    sups, blk_count, nb = factors.shape[0], panels.shape[0], member.shape[1]
    width = panels.shape[2]
    n, wide_count = lax.axis_size("narrow"), lax.axis_size("wide")
    q_count = wide_count // CORES
    tile_count = ancestors.shape[0] * wide_count
    assert ancestors.shape[0] == 1 and n % (CORES * sups) == 0 and CORES == 2 and nb % 2 == 0 and sups == 2
    unit = n // (CORES * sups)
    split = unit * CORES
    part = panels.shape[1] // split
    wide, z = lax.axis_index("wide"), lax.axis_index("narrow")
    own_members = lax.dynamic_slice_in_dim(member, wide * sups, sups, 0) - wide * blk_count
    blocks = panels[own_members]
    supernode = (wide // CORES) * (CORES * sups) + z // unit
    own_targets = lax.dynamic_slice_in_dim(target, supernode, 1, 0)
    weight = (own_targets == jnp.arange(tile_count, dtype=jnp.int32)[:, None]).astype(jnp.float32)
    units = CORES * sups
    cols = width // units
    f32, bf16 = jnp.float32, jnp.bfloat16
    dma = pltpu.SemaphoreType.DMA
    cfg = (n, q_count, sups, nb, width, part, unit, split)
    any_space = pl.BlockSpec(memory_space=pl.ANY)
    return pl.pallas_call(
        functools.partial(kernel, cfg),
        out_shape=jax.ShapeDtypeStruct(ancestors.shape, f32),
        in_specs=[pl.BlockSpec(memory_space=pltpu.SMEM), any_space, any_space, any_space],
        out_specs=pl.BlockSpec(memory_space=pltpu.VMEM),
        scratch_shapes=[
            pltpu.VMEM((n, nb, part, width), f32),
            pltpu.VMEM((n, split, part, width), f32),
            pltpu.VMEM((width, width), bf16),
            pltpu.VMEM((width, width), bf16),
            pltpu.VMEM((nb, n, split, part, width), f32),
            pltpu.VMEM((nb, n, split, part, width), bf16),
            pltpu.VMEM((nb, n, split, part, width), bf16),
            pltpu.VMEM((nb * unit * part, nb * cols), f32),
            pltpu.VMEM((units, units, tile_count, unit * part, cols), f32),
            pltpu.VMEM((q_count, units, units, CORES, unit * part, cols), f32),
            pltpu.VMEM((n, CORES, part, width), f32),
            pltpu.VMEM((n, CORES, part, width), f32),
            dma,
            dma((sups * split,)), dma((n,)),
            dma((split,)), dma((split,)),
            dma((sups * split,)), dma((n,)),
            dma((n, split)), dma((n, split)),
            dma((q_count, units, units)), dma((q_count, units, units)),
            dma((n, CORES)), dma((n, CORES)),
            pltpu.SemaphoreType.REGULAR,
        ],
        compiler_params=pltpu.CompilerParams(
            collective_id=0, has_side_effects=True, vmem_limit_bytes=58 * 2**20
        ),
        name="level",
    )(weight, blocks, factors, ancestors)


def solution(mesh):
    return jax.shard_map(
        shards,
        mesh=mesh,
        in_specs=(
            P("wide", "narrow", None),
            P("wide", "narrow", None),
            P(),
            P(),
            P("wide", "narrow", None),
        ),
        out_specs=P("wide", "narrow", None),
        check_vma=False,
    )
```

time: 135 us -> 106 us (0.79)
  Pallas kernels: 129 us -> 99.7 us
    pallas_call x1, Pallas kernels: 129 us -> 99.7 us  [shards(): pl.pallas_call(functools.partial(kernel, cfg), out_shape=jax.ShapeDtypeSt...]
where the time goes in v2:
time: 106 us
  Pallas kernels  99.7 us (94%)
  local copies, waits for them, and re-layouts  4.72 us (4%)
  other arithmetic  1.36 us (1%)
    pallas_call x1, Pallas kernels, shards(): pl.pallas_call(functools.partial(kernel, cfg), out_shape=jax.ShapeDtypeSt...  99.7 us

profile of v2, /device:TPU:1, one launch (start us, length us, event | category | flops | bytes accessed | tf_op | source)
XLA Modules:
  0.0 105.8 jit_solution(11158928329794487560)
XLA Ops:
  0.0 0.0 copy-start
  0.0 0.8 dynamic-slice_bitcast_fusion
  0.8 0.8 compare_select_fusion
  1.6 0.1 copy.6
  1.7 0.1 reshape.2
  1.8 0.6 fusion.weight
  2.4 0.0 copy-done
  2.4 2.0 %gather_fusion = f32[8,128,512]{2,1,0:T(8,128)} fusion(f32[8,128,512]{2,1,0:T(8,128)S(1)} %copy-done, s32[1024]{0:T(1024)S(1)} %pad_clamp_fusion), kind=kCustom, calls=%fused_computation | custom fusion | bytes 4194336 | tf_op jit(solution)/shard_map/gather | solution.py:293
  4.4 99.7 %level.1 = f32[1,128,512]{2,1,0:T(8,128)} custom-call(f32[8,10]{1,0:T(8,128)} %fusion.weight, f32[2,4,128,512]{3,2,1,0:T(8,128)} %bitcast.3, f32[2,128,512]{2,1,0:T(8,128)} %factors.1, f32[1,128,512]{2,1,0:T(8,128)} %ancestors.1), custom_call_target="tpu_custom_call" | custom-call | tf_op jit(solution)/shard_map/level/pallas_call | solution.py:303
  104.1 1.7 %copy.8 = f32[1,128,512]{2,1,0:T(8,128)} copy(f32[1,128,512]{2,1,0:T(8,128)} %level.1) | data formatting | bytes 524288
  (1 shorter events, 0.0 us)
Async XLA Ops:
  0.0 2.4 %copy-start = (f32[8,128,512]{2,1,0:T(8,128)S(1)}, f32[8,128,512]{2,1,0:T(8,128)}, u32[]{:S(2)}) copy-start(f32[8,128,512]{2,1,0:T(8,128)} %param.5) | copy-start | bytes 6291460

commit v3 on v2

--- a/solution.py
+++ b/solution.py
@@ -25,9 +25,9 @@
     return dot(ah, bh) + (dot(ah, bl) + dot(al, bh))
 
 
-def kernel(cfg, weight, blocks, factors, ancestors, out, p_recv, f_full, fh, fl, s_full, s_hi, s_lo,
+def kernel(cfg, member, target, panels, factors, ancestors, out, weight, held, blocks, p_recv, f_full, fh, fl, s_full, s_hi, s_lo,
            upd, portion, xy_recv, zsum, z_recv, loc_sem, fs_sem, fr_sem, f2s_sem, f2r_sem, ps_sem, pr_sem,
-           ss_sem, sr_sem, xs_sem, xr_sem, zs_sem, zr_sem, turn_sem):
+           ss_sem, sr_sem, xs_sem, xr_sem, zs_sem, zr_sem, turn_sem, held_sem):
     n, q_count, sups, nb, width, part, unit, split = cfg
     units = CORES * sups
     mid = units // 2
@@ -51,6 +51,9 @@
         far = mid + j - half * (1 + 2 * j)
         return (1 - h) * near + h * far
 
+    held_copy = pltpu.make_async_copy(panels, held, held_sem)
+    held_copy.start()
+
     barrier = pltpu.get_barrier_semaphore()
     for i in range(1, CORES * n):
         other = lax.rem(z * CORES + core + i, CORES * n)
@@ -98,7 +101,24 @@
     outer_far = jnp.logical_and(far_sender, my_unit == outer_unit)
     inner_far = jnp.logical_and(far_sender, inner)
     send_all("f")
+    held_copy.wait()
+
+    def pick(i, carry):
+        s, k = i // nb, i % nb
+        blocks[s, k] = held[lax.rem(member[wide * sups + s, k], sups * nb)]
+        return carry
+
+    lax.fori_loop(0, sups * nb, pick, 0)
     pl.when(jnp.logical_not(outer_far))(lambda: send_all("p"))
+
+    supernode = q * units + my_unit
+
+    def weigh(tile, carry):
+        for p in range(nb * (nb + 1) // 2):
+            weight[tile, p] = jnp.where(target[supernode, p] == tile, jnp.float32(1), jnp.float32(0))
+        return carry
+
+    lax.fori_loop(0, q_count * CORES, weigh, 0)
 
     def arrived(ref, sem):
         pltpu.make_async_copy(ref, ref, sem).wait()
@@ -188,7 +208,7 @@
         if i == mid:
             @pl.when(inner_far)
             def _():
-                for j in range(sups * split):
+                for j in range(sups * split - 1):
                     source_copy("p", j, False).wait_send()
                 pl.semaphore_signal(turn_sem, inc=1, device_id=at(q, core, z - unit + 2 * unit * half),
                                     device_id_type=MESH)
@@ -202,9 +222,12 @@
         scale(new)
 
         def blocks_of(j, carry, i=i, new=new):
-            old = jnp.minimum(j, i)
-            row = order(old)
-            block(row, order(jnp.where(j < i, i, j - i)))
+            ahead = i - mid if i == units - 1 else i
+            rest = j - ahead - (i + 1)
+            old = mid + j if i == units - 1 else j
+            row = jnp.where(j < ahead, old, jnp.where(rest < 0, i, mid - 1 - rest))
+            col = jnp.where(jnp.logical_and(j >= ahead, rest < 0), j - ahead, i)
+            block(order(row), order(col))
             return carry
 
         lax.fori_loop(0, 2 * i + 1, blocks_of, 0)
@@ -213,7 +236,7 @@
         return remote(zsum.at[zz, c], z_recv.at[z, core], zs_sem.at[zz, c], zr_sem.at[z, core], at(q, c, zz))
 
     def gather(i, carry):
-        a = order(i)
+        a = order(jnp.where(i < mid, mid + i, units - 1 - i))
         for b in range(units):
             total = portion[a, b, pl.ds(q * CORES, CORES)]
             for j in range(1, q_count):
@@ -253,7 +276,9 @@
         def _():
             source_copy("f", i, False).wait_send()
 
-        @pl.when(jnp.logical_not(jnp.logical_or(to_self(i), inner_far)))
+        done = jnp.logical_or(to_self(i), inner_far) if i < sups * split - 1 else to_self(i)
+
+        @pl.when(jnp.logical_not(done))
         def _():
             source_copy("p", i, False).wait_send()
     for copy in f_copies:
@@ -279,21 +304,16 @@
 
 
 def shards(panels, factors, member, target, ancestors):
-    sups, blk_count, nb = factors.shape[0], panels.shape[0], member.shape[1]
+    sups, nb = factors.shape[0], member.shape[1]
     width = panels.shape[2]
     n, wide_count = lax.axis_size("narrow"), lax.axis_size("wide")
     q_count = wide_count // CORES
     tile_count = ancestors.shape[0] * wide_count
     assert ancestors.shape[0] == 1 and n % (CORES * sups) == 0 and CORES == 2 and nb % 2 == 0 and sups == 2
+    assert panels.shape[0] == sups * nb
     unit = n // (CORES * sups)
     split = unit * CORES
     part = panels.shape[1] // split
-    wide, z = lax.axis_index("wide"), lax.axis_index("narrow")
-    own_members = lax.dynamic_slice_in_dim(member, wide * sups, sups, 0) - wide * blk_count
-    blocks = panels[own_members]
-    supernode = (wide // CORES) * (CORES * sups) + z // unit
-    own_targets = lax.dynamic_slice_in_dim(target, supernode, 1, 0)
-    weight = (own_targets == jnp.arange(tile_count, dtype=jnp.int32)[:, None]).astype(jnp.float32)
     units = CORES * sups
     cols = width // units
     f32, bf16 = jnp.float32, jnp.bfloat16
@@ -303,9 +323,12 @@
     return pl.pallas_call(
         functools.partial(kernel, cfg),
         out_shape=jax.ShapeDtypeStruct(ancestors.shape, f32),
-        in_specs=[pl.BlockSpec(memory_space=pltpu.SMEM), any_space, any_space, any_space],
+        in_specs=[pl.BlockSpec(memory_space=pltpu.SMEM)] * 2 + [any_space] * 3,
         out_specs=pl.BlockSpec(memory_space=pltpu.VMEM),
         scratch_shapes=[
+            pltpu.SMEM((tile_count, target.shape[1]), f32),
+            pltpu.VMEM(panels.shape, f32),
+            pltpu.VMEM((sups, nb) + panels.shape[1:], f32),
             pltpu.VMEM((n, nb, part, width), f32),
             pltpu.VMEM((n, split, part, width), f32),
             pltpu.VMEM((width, width), bf16),
@@ -326,12 +349,13 @@
             dma((q_count, units, units)), dma((q_count, units, units)),
             dma((n, CORES)), dma((n, CORES)),
             pltpu.SemaphoreType.REGULAR,
+            dma,
         ],
         compiler_params=pltpu.CompilerParams(
             collective_id=0, has_side_effects=True, vmem_limit_bytes=58 * 2**20
         ),
         name="level",
-    )(weight, blocks, factors, ancestors)
+    )(member, target, panels, factors, ancestors)
 
 
 def solution(mesh):

time: 106 us -> 114 us (1.075)
  Pallas kernels: 99.7 us -> 111 us
  local copies, waits for them, and re-layouts: 4.72 us -> 3.03 us
  other arithmetic: 1.36 us -> 0 us
    pallas_call x1, Pallas kernels: 99.7 us -> 111 us  [shards(): pl.pallas_call(functools.partial(kernel, cfg), out_shape=jax.ShapeDtypeSt...]
    gather x1 -> x0, local copies, waits for them, and re-layouts: 2.03 us -> none  [shards(): blocks = panels[own_members]]
    unnamed x3 -> x2, local copies, waits for them, and re-layouts: 1.68 us -> 3.03 us
where the time goes in v3:
time: 114 us
  Pallas kernels  111 us (97%)
  local copies, waits for them, and re-layouts  3.03 us (3%)
    pallas_call x1, Pallas kernels, shards(): pl.pallas_call(functools.partial(kernel, cfg), out_shape=jax.ShapeDtypeSt...  111 us
    unnamed x2, local copies, waits for them, and re-layouts  3.03 us

profile of v3, /device:TPU:1, one launch (start us, length us, event | category | flops | bytes accessed | tf_op | source)
XLA Modules:
  0.0 114.1 jit_solution(6425600878270255111)
XLA Ops:
  0.0 1.4 %copy.6.member = s32[16,4]{1,0:T(8,128)} copy(s32[16,4]{0,1:T(4,128)} %param.7) | data formatting | bytes 512 | tf_op args[2]
  1.4 111.1 %level.1 = f32[1,128,512]{2,1,0:T(8,128)} custom-call(s32[16,4]{1,0:T(8,128)} %copy.6.member, s32[16,10]{1,0:T(8,128)} %target.1, f32[8,128,512]{2,1,0:T(8,128)} %panels.1, f32[2,128,512]{2,1,0:T(8,128)} %factors.1, f32[1,128,512]{2,1,0:T(8,128)} %ancestors.1), custom_call_target="tpu_custom_call" | custom-call | tf_op jit(solution)/shard_map/level/pallas_call | solution.py:323
  112.4 1.7 %copy.8 = f32[1,128,512]{2,1,0:T(8,128)} copy(f32[1,128,512]{2,1,0:T(8,128)} %level.1) | data formatting | bytes 524288
